TPU v7x, 32 devices: a whole 2x2x4 slice. The times are simulated.
32 devices in a mesh: gx: 8 (over y, x, core), gy: 4 (over z).
Axes of the slice: x: 2, y: 2, z: 4, core: 2. Of those that a mesh axis runs over, the one named last changes fastest.
Arguments:
- probes: bfloat16 [256, 1024, 256], P('gx', 'gy'), may hold values from -6 to 6
- blk_rows: int32 [1024, 128], P(('gx', 'gy')), may hold values from 0 to 8191
- blk_sensor: int32 [1024], P(('gx', 'gy')), may hold values from 0 to 255, as said below
- blk_count: int32 [32], P(('gx', 'gy')), may hold values from 16 to 32, as said below
- coef: bfloat16 [1024, 128], P(('gx', 'gy')), may hold values from -5 to 5
- owner: int32 [256], replicated, may hold values from 0 to 31, as said below
- weights: float32 [256], replicated, may hold values from 0.1 to 1
Outputs:
- sensitivity: float32 [256], P(('gx', 'gy'))
- new_weights: float32 [256], replicated
- density: float32 [256, 1024], P('gx', 'gy')
Inputs may be any that keep to these rules, and one draw needn't show every extreme that they name: `owner`: every device owns exactly 8 sensors. `blk_sensor`: among the live slots of one tile, at most 2 belong to sensors of one owner; in every draw some owner receives 2 live blocks from every tile. `blk_count`: some tile has all 32 slots live.
All inputs are finite; a program needn't handle non-finite values.
Results may differ from a plain program's by a relative error of at most 0.0008.
Values may be sent and summed in bfloat16 or wider, within the bound.
A program may use at most 128 MiB of HBM per device.

v0:
```python
import functools

import jax
import jax.numpy as jnp
from jax import lax
from jax.experimental import pallas as pl
from jax.experimental.pallas import tpu as pltpu
from jax.sharding import PartitionSpec as P

MESH = pl.DeviceIdType.MESH
F32 = jnp.float32
BF16 = jnp.bfloat16
NT = (((1,), (1,)), ((), ()))
LANES = 128


def step_kernel(
    n, n_gy, scale,
    rows_sm, count_sm, probes_hbm, sensor_ref, rows_ref, coef_ref, owner_ref, weights_ref,
    owned_ref, new_ref, density_ref,
    probes_ref, tile_ref, stage_ref, coef32_ref, send_ref, recv_ref, ids_send, ids_recv,
    obs_ref, planes_ref, h_send, h_recv,
    load_sem, send_sem, recv_sem, ids_send_sem, ids_recv_sem, h_send_sem, h_recv_sem,
    *merge_refs,
):
    m, hz = n // 2, n_gy // 2
    half = lax.axis_index("gy") // hz
    inner = lax.axis_index("gx") * hz + lax.rem(lax.axis_index("gy"), hz)
    me = half * m + inner
    flat = lax.axis_index("gx") * n_gy + lax.axis_index("gy")
    nblk, width = send_ref.shape[1:]
    tile_r, tile_c, probe_n = probes_ref.shape
    chans = width // probe_n
    merge = bool(merge_refs)
    if merge:
        (send_m, recv_m, obs_m, part_send, part_recv,
         send_m_sem, recv_m_sem, part_send_sem, part_recv_sem) = merge_refs
        chans_m = send_m.shape[2] // probe_n
        side = part_send.shape[1]
    else:
        chans_m = 0
    n_sens = owner_ref.shape[1]
    foot = coef_ref.shape[1]
    wide = ids_send.shape[1]
    share = wide // nblk

    def device_of(t):
        q = lax.rem(t, m)
        return (q // hz, (t // m) * hz + lax.rem(q, hz))

    def peer(k):
        t = lax.rem(me + k, n)
        return t, device_of(t)

    barrier = pltpu.get_barrier_semaphore()

    def greet(k, carry):
        pl.semaphore_signal(barrier, inc=1, device_id=peer(k)[1], device_id_type=MESH)
        return carry

    parts = load_sem.shape[0]
    span = tile_r // parts

    def load(q):
        at = pl.ds(q * span, span)
        return pltpu.make_async_copy(probes_hbm.at[at], probes_ref.at[at], load_sem.at[q])

    for q in range(parts):
        load(q).start()
    lax.fori_loop(1, n, greet, 0)

    coef32_ref[...] = coef_ref[...].astype(F32)
    slot = lax.broadcasted_iota(jnp.int32, (1, nblk), 1)
    ids_one = jnp.where(slot < count_sm[0], sensor_ref[...] + 1, 0).astype(F32)
    down = lax.broadcasted_iota(jnp.int32, (nblk, nblk), 0)
    ids_col = jnp.sum(
        jnp.where(down == lax.broadcasted_iota(jnp.int32, (nblk, nblk), 1), ids_one, 0.0),
        axis=1, keepdims=True,
    )
    offset = lax.rem(me, share) * nblk
    ids_send[...] = jnp.sum(
        jnp.where(
            lax.broadcasted_iota(jnp.int32, (nblk, wide), 1)
            == lax.broadcasted_iota(jnp.int32, (nblk, wide), 0) + offset,
            ids_col, 0.0,
        ),
        axis=0, keepdims=True,
    )
    ids_recv[me] = ids_send[...]

    for q in range(parts):
        load(q).wait()

        def widen(i, carry):
            at = pl.multiple_of(i * tile_c, tile_c)
            tile_ref[pl.ds(at, tile_c), :] = probes_ref[i].astype(F32)
            return carry

        lax.fori_loop(q * span, (q + 1) * span, widen, 0)

    pl.semaphore_wait(barrier, n - 1)

    def block_copy(t):
        return pltpu.make_async_remote_copy(
            src_ref=send_ref.at[t], dst_ref=recv_ref.at[me],
            send_sem=send_sem.at[t], recv_sem=recv_sem.at[me],
            device_id=device_of(t), device_id_type=MESH,
        )

    def merge_copy(q):
        return pltpu.make_async_remote_copy(
            src_ref=send_m.at[q], dst_ref=recv_m.at[inner],
            send_sem=send_m_sem.at[q], recv_sem=recv_m_sem.at[inner],
            device_id=device_of(half * m + q), device_id_type=MESH,
        )

    def part_copy():
        return pltpu.make_async_remote_copy(
            src_ref=part_send, dst_ref=part_recv,
            send_sem=part_send_sem, recv_sem=part_recv_sem,
            device_id=device_of((1 - half) * m + inner), device_id_type=MESH,
        )

    def ids_copy(k):
        return pltpu.make_async_remote_copy(
            src_ref=ids_send, dst_ref=ids_recv.at[me],
            send_sem=ids_send_sem.at[k], recv_sem=ids_recv_sem.at[me],
            device_id=peer(k)[1], device_id_type=MESH,
        )

    def h_copy(k):
        return pltpu.make_async_remote_copy(
            src_ref=h_send, dst_ref=h_recv.at[me],
            send_sem=h_send_sem.at[k], recv_sem=h_recv_sem.at[me],
            device_id=peer(k)[1], device_id_type=MESH,
        )

    channel = lax.broadcasted_iota(jnp.int32, (nblk, foot), 1)

    def gather(dst, d, first, count, base):
        for c in range(count):
            r = first + c
            for j in range(nblk):
                i = rows_sm[j, r]
                stage_ref[base + c, pl.ds(j, 1), :] = tile_ref[pl.ds(i, 1), :]
            column = jnp.sum(
                jnp.where(channel == r, coef32_ref[...], 0.0), axis=1, keepdims=True
            )
            dst[d, :, c * probe_n : (c + 1) * probe_n] = (stage_ref[base + c] * column).astype(BF16)

    def inside(k):
        return lax.rem(inner + k, m)

    def ids_launch(k, carry):
        ids_copy(k).start()
        return carry

    lax.fori_loop(1, n, ids_launch, 0)

    def launch_first(k, carry):
        q = inside(k)
        t = (1 - half) * m + q
        if merge:
            gather(send_m, q, q * chans_m, chans_m, 0)
        gather(send_ref, t, m * chans_m + t * chans, chans, chans_m)

        @pl.when(k > 1)
        def _():
            if merge:
                merge_copy(inside(k - 1)).start()
            block_copy((1 - half) * m + inside(k - 1)).start()

        return carry

    lax.fori_loop(1, m + 1, launch_first, 0)

    def launch_second(k, carry):
        t = half * m + inside(k)
        gather(send_ref, t, m * chans_m + t * chans, chans, 0)

        @pl.when(k == 1)
        def _():
            block_copy((1 - half) * m + inner).start()

        @pl.when(k > 1)
        def _():
            block_copy(half * m + inside(k - 1)).start()

        return carry

    lax.fori_loop(1, m + 1, launch_second, 0)
    own = pltpu.make_async_copy(send_ref.at[me], recv_ref.at[me], recv_sem.at[me])
    if merge:
        own_m = pltpu.make_async_copy(send_m.at[inner], recv_m.at[inner], recv_m_sem.at[inner])
        own_m.start()

    def plane(j, carry):
        at = rows_ref[pl.ds(j, 1), :]
        c = coef32_ref[pl.ds(j, 1), :]
        square = c * c
        top = square.astype(BF16).astype(F32)
        high = at // tile_c
        low = at - high * tile_c
        here = high == lax.broadcasted_iota(jnp.int32, (tile_r, foot), 0)
        left = jnp.concatenate(
            [jnp.where(here, top, 0.0), jnp.where(here, square - top, 0.0)], axis=0
        ).astype(BF16)
        right = jnp.where(
            low == lax.broadcasted_iota(jnp.int32, (tile_c, foot), 0), 1.0, 0.0
        ).astype(BF16)
        both = lax.dot_general(left, right, NT, preferred_element_type=F32)
        planes_ref[j] = both[:tile_r] + both[tile_r:]
        return carry

    lax.fori_loop(0, nblk, plane, 0)
    own.start()

    spd = n_sens // n
    mine = jnp.where(owner_ref[...] == flat, 1.0, 0.0)
    before = jnp.where(
        lax.broadcasted_iota(jnp.int32, (n_sens, n_sens), 0)
        < lax.broadcasted_iota(jnp.int32, (n_sens, n_sens), 1),
        1.0, 0.0,
    ).astype(BF16)
    rank = jnp.dot(
        jnp.broadcast_to(mine, (spd, n_sens)).astype(BF16), before, preferred_element_type=F32
    )
    place = lax.broadcasted_iota(jnp.int32, (spd, n_sens), 0).astype(F32)
    select = jnp.where(rank == place, 1.0, 0.0) * mine

    def ids_wait(k, carry):
        t = peer(k)[0]
        pltpu.make_async_copy(ids_send, ids_recv.at[t], ids_recv_sem.at[t]).wait()
        return carry

    lax.fori_loop(1, n, ids_wait, 0)

    group = max(1, 256 // nblk)
    depth = group * nblk
    sensor_up = (lax.broadcasted_iota(jnp.int32, (n_sens, depth), 0) + 1).astype(F32)

    def mix(src, sem, like, obs, start, g):
        pieces = []
        for piece in range(depth // wide):
            row = ids_recv[start + g * group + piece * share]
            for extra in range(1, share):
                row = row + ids_recv[start + g * group + piece * share + extra]
            pieces.append(row)
        ids_row = jnp.concatenate(pieces, axis=1)
        mixer = jnp.where(ids_row == sensor_up, 1.0, 0.0).astype(BF16)
        for piece in range(group):
            t = g * group + piece
            pltpu.make_async_copy(like, src.at[t], sem.at[t]).wait()
        block = src[pl.ds(g * group, group)].reshape(depth, src.shape[2])
        obs[...] += jnp.dot(mixer, block, preferred_element_type=F32)

    obs_ref[...] = jnp.zeros_like(obs_ref)
    if merge:
        obs_m[...] = jnp.zeros_like(obs_m)

        def mix_m(g, carry):
            mix(recv_m, recv_m_sem, send_m.at[0], obs_m, half * m, g)
            return carry

        lax.fori_loop(0, m // group, mix_m, 0)
        away = pl.multiple_of((1 - half) * side, LANES)
        part_send[...] = obs_m[:, pl.ds(away, side)].astype(BF16)
        part_copy().start()

    def mix_d(g, carry):
        mix(recv_ref, recv_sem, send_ref.at[0], obs_ref, 0, g)
        return carry

    lax.fori_loop(0, n // group, mix_d, 0)
    if merge:
        part_copy().wait()
        keep = pl.multiple_of(half * side, LANES)

    eye = lax.broadcasted_iota(jnp.int32, (LANES, LANES), 0) == lax.broadcasted_iota(
        jnp.int32, (LANES, LANES), 1
    )
    for b in range(n_sens // LANES):
        x = obs_ref[b * LANES : (b + 1) * LANES, :]
        s = jnp.sum(x * x, axis=1, keepdims=True)
        if merge:
            rows = pl.ds(b * LANES, LANES)
            y = obs_m[rows, pl.ds(keep, side)] + part_recv[rows, :].astype(F32)
            s = s + jnp.sum(y * y, axis=1, keepdims=True)
        h_send[:, b * LANES : (b + 1) * LANES] = jnp.sum(
            jnp.where(eye, s, 0.0), axis=0, keepdims=True
        )
    h_recv[me] = h_send[...]

    def h_launch(k, carry):
        h_copy(k).start()
        return carry

    lax.fori_loop(1, n, h_launch, 0)

    def drain(k, carry):
        block_copy(peer(k)[0]).wait_send()
        ids_copy(k).wait_send()
        return carry

    lax.fori_loop(1, n, drain, 0)
    if merge:

        def drain_m(k, carry):
            merge_copy(inside(k)).wait_send()
            return carry

        lax.fori_loop(1, m, drain_m, 0)

    def h_wait(k, carry):
        t = peer(k)[0]
        pltpu.make_async_copy(h_send, h_recv.at[t], h_recv_sem.at[t]).wait()
        return carry

    lax.fori_loop(1, n, h_wait, 0)
    h = jnp.sum(h_recv[...], axis=0) * scale
    gain = weights_ref[...] * jnp.sqrt(1.0 + h)
    new = n_sens * gain / jnp.sum(gain, axis=1, keepdims=True)
    new_ref[...] = new
    owned = jnp.sum(select * h, axis=1, keepdims=True)
    small = lax.broadcasted_iota(jnp.int32, (spd, spd), 0) == lax.broadcasted_iota(
        jnp.int32, (spd, spd), 1
    )
    owned_ref[...] = jnp.sum(jnp.where(small, owned, 0.0), axis=0, keepdims=True)
    lookup = ids_col == (lax.broadcasted_iota(jnp.int32, (nblk, n_sens), 1) + 1).astype(F32)
    factor = jnp.sum(jnp.where(lookup, new, 0.0), axis=1, keepdims=True)
    total = factor[0:1] * planes_ref[0]
    for j in range(1, nblk):
        total = total + factor[j : j + 1] * planes_ref[j]
    density_ref[...] = total

    def h_drain(k, carry):
        h_copy(k).wait_send()
        return carry

    lax.fori_loop(1, n, h_drain, 0)


def local(n, n_gy, probes, blk_rows, blk_sensor, blk_count, coef, owner, weights):
    tile_r, tile_c, probe_n = probes.shape
    nblk, foot = blk_rows.shape
    n_sens = owner.shape[0]
    merge = foot % (2 * n) == 0
    chans = foot // (2 * n) if merge else foot // n
    chans_m = 2 * chans if merge else 0
    width = chans * probe_n
    wide = max(LANES, nblk)

    vmem = pl.BlockSpec(memory_space=pltpu.VMEM)
    smem = pl.BlockSpec(memory_space=pltpu.SMEM)
    dma = pltpu.SemaphoreType.DMA
    merge_scratch = []
    if merge:
        m = n // 2
        merge_scratch = [
            pltpu.VMEM((m, nblk, chans_m * probe_n), BF16),
            pltpu.VMEM((m, nblk, chans_m * probe_n), BF16),
            pltpu.VMEM((n_sens, chans_m * probe_n), F32),
            pltpu.VMEM((n_sens, width), BF16),
            pltpu.VMEM((n_sens, width), BF16),
            dma((m,)), dma((m,)), dma, dma,
        ]
    owned, new, density = pl.pallas_call(
        functools.partial(step_kernel, n, n_gy, 1.0 / (foot * probe_n)),
        out_shape=(
            jax.ShapeDtypeStruct((1, n_sens // n), F32),
            jax.ShapeDtypeStruct((1, n_sens), F32),
            jax.ShapeDtypeStruct((tile_r, tile_c), F32),
        ),
        in_specs=[smem, smem, pl.BlockSpec(memory_space=pltpu.HBM)] + [vmem] * 5,
        out_specs=(vmem, vmem, vmem),
        scratch_shapes=[
            pltpu.VMEM((tile_r, tile_c, probe_n), BF16),
            pltpu.VMEM((tile_r * tile_c, probe_n), F32),
            pltpu.VMEM((chans + chans_m, nblk, probe_n), F32),
            pltpu.VMEM((nblk, foot), F32),
            pltpu.VMEM((n, nblk, width), BF16),
            pltpu.VMEM((n, nblk, width), BF16),
            pltpu.VMEM((1, wide), F32),
            pltpu.VMEM((n, 1, wide), F32),
            pltpu.VMEM((n_sens, width), F32),
            pltpu.VMEM((nblk, tile_r, tile_c), F32),
            pltpu.VMEM((1, n_sens), F32),
            pltpu.VMEM((n, 1, n_sens), F32),
            dma((4,)), dma((n,)), dma((n,)), dma((n,)), dma((n,)), dma((n,)), dma((n,)),
        ] + merge_scratch,
        compiler_params=pltpu.CompilerParams(
            collective_id=0, has_side_effects=True, vmem_limit_bytes=56 * 2**20
        ),
        name="reweight_step",
    )(
        blk_rows, blk_count, probes, blk_sensor.reshape(1, nblk), blk_rows, coef,
        owner.reshape(1, n_sens), weights.reshape(1, n_sens),
    )
    return owned.reshape(-1), new.reshape(-1), density


def solution(mesh):
    n_gy = mesh.shape["gy"]
    n = mesh.shape["gx"] * n_gy
    in_specs = (
        P("gx", "gy", None),
        P(("gx", "gy"), None),
        P(("gx", "gy")),
        P(("gx", "gy")),
        P(("gx", "gy"), None),
        P(),
        P(),
    )
    out_specs = (P(("gx", "gy")), P(), P("gx", "gy"))
    return jax.shard_map(
        functools.partial(local, n, n_gy),
        mesh=mesh, in_specs=in_specs, out_specs=out_specs, check_vma=False,
    )
```

profile of v0, /device:TPU:0, one launch (start us, length us, event | category | flops | bytes accessed | tf_op | source)
XLA Modules:
  0.0 59.2 jit_solution(16070400400167457937)
XLA Ops:
  1.3 54.1 %reweight_step.1 = (f32[1,8]{1,0:T(1,128)}, f32[1,256]{1,0:T(1,128)}, f32[32,256]{1,0:T(8,128)}) custom-call(s32[32,128]{1,0:T(8,128)} %rows_ref.1, s32[1]{0:T(128)S(6)} %copy.13.count_sm, bf16[32,256,256]{2,1,0:T(8,128)(2,1)} %probes_hbm.1, s32[1,32]{1,0:T(1,128)} %bitcast.8, s32[32,128]{1,0:T(8,128)} %rows_ref.1, bf16[32,128]{1,0:T(8,128)(2,1)} %coef_ref.1, ...), custom_call_target="tpu_custom_call" | custom-call | tf_op jit(solution)/shard_map/reweight_step/pallas_call | solution.py:367
  55.4 1.1 %copy.14 = f32[8]{0:T(128)} copy(f32[8]{0:T(128)} %bitcast.9) | data formatting | bytes 64
  56.6 1.2 %copy.15 = f32[256]{0:T(256)} copy(f32[256]{0:T(256)} %bitcast.7) | data formatting | bytes 2048
  57.8 1.4 %copy.16 = f32[32,256]{1,0:T(8,128)} copy(f32[32,256]{1,0:T(8,128)} %get-tuple-element.14) | data formatting | bytes 65536
where the time goes:
time: 59.5 us; the launch traced here: 59.2 us
  Pallas kernels  54.1 us (91%)
  local copies, waits for them, and re-layouts  3.75 us (6%)
  between operations  1.29 us (2%)
    pallas_call x1, Pallas kernels, local(): pl.pallas_call(functools.partial(step_kernel, n, n_gy, 1.0 / (foot * prob...  54.1 us
    unnamed x3, local copies, waits for them, and re-layouts  3.75 us

commit v1 on v0

v1 whole, which is shorter than its diff:
```python
import functools

import jax
import jax.numpy as jnp
from jax import lax
from jax.experimental import pallas as pl
from jax.experimental.pallas import tpu as pltpu
from jax.sharding import PartitionSpec as P

MESH = pl.DeviceIdType.MESH
F32 = jnp.float32
BF16 = jnp.bfloat16
NT = (((1,), (1,)), ((), ()))
LANES = 128
LAG = 3
AHEAD = 3


def step_kernel(
    n_gx, n_gy, scale, tail,
    rows_hbm, probes_hbm, count_ref, sensor_ref, rows_ref, coef_ref, owner_ref, weights_ref,
    owned_ref, new_ref, density_ref,
    rows_sm, probes_ref, tile_ref, stage_ref, coef32_ref, send_ref, recv_ref, ids_send, ids_recv,
    mixer_ref, y_ref, part_out, part_in, part_x, acc_ref, planes_ref, h_send, h_recv,
    rows_sem, load_sem, send_sem, recv_sem, ids_send_sem, ids_recv_sem, part_send_sem,
    part_sem, part_x_sem, h_send_sem, h_recv_sem,
):
    n = n_gx * n_gy
    gx = lax.axis_index("gx")
    gy = lax.axis_index("gy")
    flat = gx * n_gy + gy
    items, _, nblk, width = send_ref.shape[1:]
    tile_r, tile_c, probe_n = probes_ref.shape
    split = probe_n // width
    groups = items // split
    depth_k = n_gx * nblk
    n_sens = owner_ref.shape[1]
    foot = coef_ref.shape[1]
    wide = ids_send.shape[1]
    share = wide // nblk
    first_tail = items - tail

    parts = load_sem.shape[0]
    span = tile_r // parts

    def load(q):
        at = pl.ds(q * span, span)
        return pltpu.make_async_copy(probes_hbm.at[at], probes_ref.at[at], load_sem.at[q])

    for q in range(parts):
        load(q).start()
    rows_copy = pltpu.make_async_copy(rows_hbm, rows_sm, rows_sem)
    rows_copy.start()

    def across(j):
        return (lax.rem(gx + j, n_gx), gy)

    barrier = pltpu.get_barrier_semaphore()

    def greet(j, carry):
        pl.semaphore_signal(barrier, inc=1, device_id=across(j), device_id_type=MESH)
        return carry

    lax.fori_loop(1, n_gx, greet, 0)

    @pl.when(gy > 0)
    def _():
        pl.semaphore_signal(barrier, inc=1, device_id=(gx, gy - 1), device_id_type=MESH)

    @pl.when(gy < n_gy - 1)
    def _():
        pl.semaphore_signal(barrier, inc=1, device_id=(gx, gy + 1), device_id_type=MESH)

    coef32_ref[...] = coef_ref[...].astype(F32)
    slot = lax.broadcasted_iota(jnp.int32, (1, nblk), 1)
    ids_one = jnp.where(slot < count_ref[...], sensor_ref[...] + 1, 0).astype(F32)
    down = lax.broadcasted_iota(jnp.int32, (nblk, nblk), 0)
    ids_col = jnp.sum(
        jnp.where(down == lax.broadcasted_iota(jnp.int32, (nblk, nblk), 1), ids_one, 0.0),
        axis=1, keepdims=True,
    )
    offset = lax.rem(gx, share) * nblk
    ids_send[...] = jnp.sum(
        jnp.where(
            lax.broadcasted_iota(jnp.int32, (nblk, wide), 1)
            == lax.broadcasted_iota(jnp.int32, (nblk, wide), 0) + offset,
            ids_col, 0.0,
        ),
        axis=0, keepdims=True,
    )
    ids_recv[gx] = ids_send[...]

    for q in range(parts):
        load(q).wait()

        def widen(i, carry):
            at = pl.multiple_of(i * tile_c, tile_c)
            tile_ref[pl.ds(at, tile_c), :] = probes_ref[i].astype(F32)
            return carry

        lax.fori_loop(q * span, (q + 1) * span, widen, 0)
    rows_copy.wait()

    def block_copy(q, c, j):
        return pltpu.make_async_remote_copy(
            src_ref=send_ref.at[q, c, across(j)[0]], dst_ref=recv_ref.at[q, c, gx],
            send_sem=send_sem.at[q, c], recv_sem=recv_sem.at[q, c],
            device_id=across(j), device_id_type=MESH,
        )

    def ids_copy(j):
        return pltpu.make_async_remote_copy(
            src_ref=ids_send, dst_ref=ids_recv.at[gx],
            send_sem=ids_send_sem.at[j], recv_sem=ids_recv_sem.at[gx],
            device_id=across(j), device_id_type=MESH,
        )

    def part_copy(q, c, up):
        return pltpu.make_async_remote_copy(
            src_ref=part_out.at[q, c], dst_ref=part_in.at[q, c],
            send_sem=part_send_sem.at[q, c], recv_sem=part_sem.at[q, c],
            device_id=(gx, gy + up), device_id_type=MESH,
        )

    def part_x_copy(q, c, up):
        return pltpu.make_async_remote_copy(
            src_ref=part_out.at[q, c], dst_ref=part_x.at[q, c - first_tail],
            send_sem=part_send_sem.at[q, c], recv_sem=part_x_sem.at[q, c - first_tail],
            device_id=(gx, gy + up), device_id_type=MESH,
        )

    def h_peer(k):
        t = lax.rem(flat + k, n)
        return t, (t // n_gy, lax.rem(t, n_gy))

    def h_copy(k):
        return pltpu.make_async_remote_copy(
            src_ref=h_send, dst_ref=h_recv.at[flat],
            send_sem=h_send_sem.at[k], recv_sem=h_recv_sem.at[flat],
            device_id=h_peer(k)[1], device_id_type=MESH,
        )

    channel = lax.broadcasted_iota(jnp.int32, (nblk, foot), 1)
    batch = stage_ref.shape[0]

    def gather(g):
        for q in range(2):
            def some(b, carry):
                for e in range(batch):
                    d = b * batch + e
                    r = (g * 2 + q) * n_gx + d
                    for j in range(nblk):
                        stage_ref[e, pl.ds(j, 1), :] = tile_ref[pl.ds(rows_sm[j, r], 1), :]
                    column = jnp.sum(
                        jnp.where(channel == r, coef32_ref[...], 0.0), axis=1, keepdims=True
                    )
                    block = (stage_ref[e] * column).astype(BF16)
                    for p in range(split):
                        send_ref[q, g * split + p, d] = block[:, p * width : (p + 1) * width]
                return carry

            lax.fori_loop(0, n_gx // batch, some, 0)

    def launch(g):
        for p in range(split):
            for q in range(2):
                c = g * split + p
                recv_ref[q, c, gx] = send_ref[q, c, gx]
                for j in range(1, n_gx):
                    block_copy(q, c, j).start()

    gather(0)
    pl.semaphore_wait(
        barrier,
        n_gx - 1 + jnp.where(gy > 0, 1, 0) + jnp.where(gy < n_gy - 1, 1, 0),
    )
    for j in range(1, n_gx):
        ids_copy(j).start()
    launch(0)

    def gather_on(g, carry):
        gather(g)
        launch(g)
        return carry

    lax.fori_loop(1, AHEAD, gather_on, 0)

    for j in range(1, n_gx):
        t = across(j)[0]
        pltpu.make_async_copy(ids_send, ids_recv.at[t], ids_recv_sem.at[t]).wait()
    sensor_up = (lax.broadcasted_iota(jnp.int32, (n_sens, wide), 0) + 1).astype(F32)
    for piece in range(n_gx // share):
        row = ids_recv[piece * share]
        for extra in range(1, share):
            row = row + ids_recv[piece * share + extra]
        mixer_ref[:, piece * wide : (piece + 1) * wide] = jnp.where(
            row == sensor_up, 1.0, 0.0
        ).astype(BF16)
    acc_ref[...] = jnp.zeros_like(acc_ref)

    others = pl.ds(0, n_gx - 1)

    def process(q, c, f, crossing):
        pltpu.make_async_copy(
            send_ref.at[q, c, others], recv_ref.at[q, c, others], recv_sem.at[q, c]
        ).wait()
        y_ref[...] = jnp.dot(
            mixer_ref[...], recv_ref[q, c].reshape(depth_k, width), preferred_element_type=F32
        )
        below = (gy > 0) & (gy <= f)
        above = (gy < n_gy - 1) & (gy >= f)

        @pl.when(below if q == 0 else above)
        def _():
            pltpu.make_async_copy(part_out.at[q, c], part_in.at[q, c], part_sem.at[q, c]).wait()
            y_ref[...] += part_in[q, c].astype(F32)

        if crossing:
            @pl.when(above if q == 0 else below)
            def _():
                at = c - first_tail
                pltpu.make_async_copy(
                    part_out.at[q, c], part_x.at[q, at], part_x_sem.at[q, at]
                ).wait()
                y_ref[...] += part_x[q, at].astype(F32)

        @pl.when(gy == f)
        def _():
            total = acc_ref[...]
            for at in range(0, width, LANES):
                y = y_ref[:, at : at + LANES]
                total = total + y * y
            acc_ref[...] = total

        @pl.when(gy < f)
        def _():
            part_out[q, c] = y_ref[...].astype(BF16)
            (part_copy if q == 0 else part_x_copy)(q, c, 1).start()

        @pl.when(gy > f)
        def _():
            part_out[q, c] = y_ref[...].astype(BF16)
            (part_copy if q == 1 else part_x_copy)(q, c, -1).start()

    def ends(q, crossing):
        if crossing:
            return n_gy // 2 - q
        return n_gy - 1 if q == 0 else 0

    def depth_of(f):
        low = jnp.where(gy <= f, gy, 0)
        high = jnp.where(gy >= f, n_gy - 1 - gy, 0)
        return jnp.maximum(low, high)

    def plane(j):
        at = rows_ref[pl.ds(j, 1), :]
        c = coef32_ref[pl.ds(j, 1), :]
        square = c * c
        top = square.astype(BF16).astype(F32)
        high = at // tile_c
        low = at - high * tile_c
        here = high == lax.broadcasted_iota(jnp.int32, (tile_r, foot), 0)
        left = jnp.concatenate(
            [jnp.where(here, top, 0.0), jnp.where(here, square - top, 0.0)], axis=0
        ).astype(BF16)
        right = jnp.where(
            low == lax.broadcasted_iota(jnp.int32, (tile_c, foot), 0), 1.0, 0.0
        ).astype(BF16)
        both = lax.dot_general(left, right, NT, preferred_element_type=F32)
        planes_ref[j] = both[:tile_r] + both[tile_r:]

    steps = items + LAG * (n_gy - 1)
    per_step = -(-nblk // items)

    def step(s, carry):
        g = s // split + AHEAD

        @pl.when((lax.rem(s, split) == 0) & (g < groups))
        def _():
            gather(g)
            launch(g)

        for crossing in (True, False):
            for q in range(2):
                f = ends(q, crossing)
                if crossing:
                    lo, hi = first_tail, items
                else:
                    lo, hi = 0, first_tail
                if lo == hi:
                    continue
                c = s - LAG * depth_of(f)

                @pl.when((c >= lo) & (c < hi))
                def _():
                    process(q, c, f, crossing)

        for e in range(per_step):
            @pl.when(s * per_step + e < nblk)
            def _():
                plane(s * per_step + e)

        return carry

    lax.fori_loop(0, steps, step, 0)

    eye = lax.broadcasted_iota(jnp.int32, (LANES, LANES), 0) == lax.broadcasted_iota(
        jnp.int32, (LANES, LANES), 1
    )
    for b in range(n_sens // LANES):
        s = jnp.sum(acc_ref[b * LANES : (b + 1) * LANES, :], axis=1, keepdims=True)
        h_send[:, b * LANES : (b + 1) * LANES] = jnp.sum(
            jnp.where(eye, s, 0.0), axis=0, keepdims=True
        )
    h_recv[flat] = h_send[...]

    def h_launch(k, carry):
        h_copy(k).start()
        return carry

    lax.fori_loop(1, n, h_launch, 0)

    spd = n_sens // n
    mine = jnp.where(owner_ref[...] == flat, 1.0, 0.0)
    before = jnp.where(
        lax.broadcasted_iota(jnp.int32, (n_sens, n_sens), 0)
        < lax.broadcasted_iota(jnp.int32, (n_sens, n_sens), 1),
        1.0, 0.0,
    ).astype(BF16)
    rank = jnp.dot(
        jnp.broadcast_to(mine, (spd, n_sens)).astype(BF16), before, preferred_element_type=F32
    )
    place = lax.broadcasted_iota(jnp.int32, (spd, n_sens), 0).astype(F32)
    select = jnp.where(rank == place, 1.0, 0.0) * mine

    def drain(c, carry):
        for q in range(2):
            pltpu.make_async_copy(
                send_ref.at[q, c, others], recv_ref.at[q, c, others], send_sem.at[q, c]
            ).wait()
            f = jnp.where(c < first_tail, ends(q, False), ends(q, True))

            @pl.when(gy != f)
            def _():
                pltpu.make_async_copy(
                    part_out.at[q, c], part_in.at[q, c], part_send_sem.at[q, c]
                ).wait()
        return carry

    lax.fori_loop(0, items, drain, 0)
    for j in range(1, n_gx):
        ids_copy(j).wait_send()

    def h_wait(k, carry):
        t = h_peer(k)[0]
        pltpu.make_async_copy(h_send, h_recv.at[t], h_recv_sem.at[t]).wait()
        return carry

    lax.fori_loop(1, n, h_wait, 0)
    h = jnp.sum(h_recv[...], axis=0) * scale
    gain = weights_ref[...] * jnp.sqrt(1.0 + h)
    new = n_sens * gain / jnp.sum(gain, axis=1, keepdims=True)
    new_ref[...] = new
    owned = jnp.sum(select * h, axis=1, keepdims=True)
    small = lax.broadcasted_iota(jnp.int32, (spd, spd), 0) == lax.broadcasted_iota(
        jnp.int32, (spd, spd), 1
    )
    owned_ref[...] = jnp.sum(jnp.where(small, owned, 0.0), axis=0, keepdims=True)
    lookup = ids_col == (lax.broadcasted_iota(jnp.int32, (nblk, n_sens), 1) + 1).astype(F32)
    factor = jnp.sum(jnp.where(lookup, new, 0.0), axis=1, keepdims=True)
    total = factor[0:1] * planes_ref[0]
    for j in range(1, nblk):
        total = total + factor[j : j + 1] * planes_ref[j]
    density_ref[...] = total

    def h_drain(k, carry):
        h_copy(k).wait_send()
        return carry

    lax.fori_loop(1, n, h_drain, 0)


def local(n_gx, n_gy, probes, blk_rows, blk_sensor, blk_count, coef, owner, weights):
    tile_r, tile_c, probe_n = probes.shape
    nblk, foot = blk_rows.shape
    n_sens = owner.shape[0]
    n = n_gx * n_gy
    width = LANES
    items = (foot // n_gx // 2) * (probe_n // width)
    tail = items // 6
    wide = max(LANES, nblk)
    batch = min(n_gx, max(1, 256 // nblk))

    vmem = pl.BlockSpec(memory_space=pltpu.VMEM)
    hbm = pl.BlockSpec(memory_space=pltpu.HBM)
    dma = pltpu.SemaphoreType.DMA
    owned, new, density = pl.pallas_call(
        functools.partial(step_kernel, n_gx, n_gy, 1.0 / (foot * probe_n), tail),
        out_shape=(
            jax.ShapeDtypeStruct((1, n_sens // n), F32),
            jax.ShapeDtypeStruct((1, n_sens), F32),
            jax.ShapeDtypeStruct((tile_r, tile_c), F32),
        ),
        in_specs=[hbm, hbm] + [vmem] * 6,
        out_specs=(vmem, vmem, vmem),
        scratch_shapes=[
            pltpu.SMEM((nblk, foot), jnp.int32),
            pltpu.VMEM((tile_r, tile_c, probe_n), BF16),
            pltpu.VMEM((tile_r * tile_c, probe_n), F32),
            pltpu.VMEM((batch, nblk, probe_n), F32),
            pltpu.VMEM((nblk, foot), F32),
            pltpu.VMEM((2, items, n_gx, nblk, width), BF16),
            pltpu.VMEM((2, items, n_gx, nblk, width), BF16),
            pltpu.VMEM((1, wide), F32),
            pltpu.VMEM((n_gx, 1, wide), F32),
            pltpu.VMEM((n_sens, n_gx * nblk), BF16),
            pltpu.VMEM((n_sens, width), F32),
            pltpu.VMEM((2, items, n_sens, width), BF16),
            pltpu.VMEM((2, items, n_sens, width), BF16),
            pltpu.VMEM((2, max(1, tail), n_sens, width), BF16),
            pltpu.VMEM((n_sens, LANES), F32),
            pltpu.VMEM((nblk, tile_r, tile_c), F32),
            pltpu.VMEM((1, n_sens), F32),
            pltpu.VMEM((n, 1, n_sens), F32),
            dma, dma((4,)), dma((2, items)), dma((2, items)), dma((n_gx,)), dma((n_gx,)),
            dma((2, items)), dma((2, items)), dma((2, max(1, tail))), dma((n,)), dma((n,)),
        ],
        compiler_params=pltpu.CompilerParams(
            collective_id=0, has_side_effects=True, vmem_limit_bytes=60 * 2**20
        ),
        name="reweight_step",
    )(
        blk_rows, probes, blk_count.reshape(1, 1), blk_sensor.reshape(1, nblk), blk_rows, coef,
        owner.reshape(1, n_sens), weights.reshape(1, n_sens),
    )
    return owned.reshape(-1), new.reshape(-1), density


def solution(mesh):
    n_gx, n_gy = mesh.shape["gx"], mesh.shape["gy"]
    in_specs = (
        P("gx", "gy", None),
        P(("gx", "gy"), None),
        P(("gx", "gy")),
        P(("gx", "gy")),
        P(("gx", "gy"), None),
        P(),
        P(),
    )
    out_specs = (P(("gx", "gy")), P(), P("gx", "gy"))
    return jax.shard_map(
        functools.partial(local, n_gx, n_gy),
        mesh=mesh, in_specs=in_specs, out_specs=out_specs, check_vma=False,
    )
```

time: 59.5 us -> 57.9 us (0.973)
  Pallas kernels: 54.1 us -> 52.6 us
    pallas_call x1, Pallas kernels: 54.1 us -> 52.6 us  [local(): pl.pallas_call(functools.partial(step_kernel, n_gx, n_gy, 1.0 / (foot * p...]
where the time goes in v1:
time: 57.9 us; the launch traced here: 57.6 us
  Pallas kernels  52.6 us (91%)
  local copies, waits for them, and re-layouts  3.75 us (6%)
  between operations  1.29 us (2%)
    pallas_call x1, Pallas kernels, local(): pl.pallas_call(functools.partial(step_kernel, n_gx, n_gy, 1.0 / (foot * p...  52.6 us
    unnamed x3, local copies, waits for them, and re-layouts  3.75 us

profile of v1, /device:TPU:0, one launch (start us, length us, event | category | flops | bytes accessed | tf_op | source)
XLA Modules:
  0.0 57.6 jit_solution(10672449306449642251)
XLA Ops:
  1.3 52.6 %reweight_step.1 = (f32[1,8]{1,0:T(1,128)}, f32[1,256]{1,0:T(1,128)}, f32[32,256]{1,0:T(8,128)}) custom-call(s32[32,128]{1,0:T(8,128)} %rows_ref.1, bf16[32,256,256]{2,1,0:T(8,128)(2,1)} %probes_hbm.1, s32[1,1]{1,0:T(1,128)} %bitcast.6.count_ref, s32[1,32]{1,0:T(1,128)} %bitcast.10, s32[32,128]{1,0:T(8,128)} %rows_ref.1, bf16[32,128]{1,0:T(8,128)(2,1)} %coef_ref.1, ...), custom_call_target="tpu_custom_call" | custom-call | tf_op jit(solution)/shard_map/reweight_step/pallas_call | solution.py:397
  53.9 1.1 %copy.14 = f32[8]{0:T(128)} copy(f32[8]{0:T(128)} %bitcast.11) | data formatting | bytes 64
  55.0 1.2 %copy.15 = f32[256]{0:T(256)} copy(f32[256]{0:T(256)} %bitcast.9) | data formatting | bytes 2048
  56.3 1.4 %copy.16 = f32[32,256]{1,0:T(8,128)} copy(f32[32,256]{1,0:T(8,128)} %get-tuple-element.14) | data formatting | bytes 65536

commit v2 on v1

v2 whole, which is shorter than its diff:
```python
import functools

import jax
import jax.numpy as jnp
from jax import lax
from jax.experimental import pallas as pl
from jax.experimental.pallas import tpu as pltpu
from jax.sharding import PartitionSpec as P

MESH = pl.DeviceIdType.MESH
F32 = jnp.float32
BF16 = jnp.bfloat16
NT = (((1,), (1,)), ((), ()))
LANES = 128
LAG = 3
STACK = 1
TAIL = 4
AHEAD = 6
FRONT = 0


def step_kernel(
    n_gx, n_gy, scale, tail,
    rows_hbm, probes_hbm, count_hbm, sensor_hbm, coef_hbm, owner_hbm, weights_hbm,
    owned_hbm, new_hbm, density_hbm,
    count_ref, sensor_ref, rows_ref, coef_ref, owner_ref, weights_ref,
    owned_ref, new_ref, density_ref, small_sem, out_sem,
    rows_sm, probes_ref, tile_ref, stage_ref, coef32_ref, send_ref, recv_ref, ids_send, ids_recv,
    mixer_ref, own_ref, part_out, part_in, part_x, acc_ref, planes_ref, h_send, h_recv,
    rows_sem, load_sem, send_sem, recv_sem, ids_send_sem, ids_recv_sem, part_send_sem,
    part_sem, part_x_sem, h_send_sem, h_recv_sem,
):
    n = n_gx * n_gy
    gx = lax.axis_index("gx")
    gy = lax.axis_index("gy")
    flat = gx * n_gy + gy
    groups, _, nblk, probe_n = send_ref.shape[1:]
    items, part_rows, width = part_in.shape[1:]
    tile_r, tile_c = probes_ref.shape[:2]
    split = probe_n // width
    stack = owner_ref.shape[1] // part_rows
    fine = split * stack
    depth_k = n_gx * nblk
    n_sens = owner_ref.shape[1]
    foot = coef_ref.shape[1]
    wide = ids_send.shape[1]
    share = wide // nblk
    first_tail = items - tail

    parts = load_sem.shape[0]
    span = tile_r // parts

    def load(q):
        at = pl.ds(q * span, span)
        return pltpu.make_async_copy(probes_hbm.at[at], probes_ref.at[at], load_sem.at[q])

    pairs = (
        (count_hbm, count_ref), (sensor_hbm, sensor_ref), (rows_hbm, rows_ref),
        (coef_hbm, coef_ref), (owner_hbm, owner_ref), (weights_hbm, weights_ref),
    )
    small = [
        pltpu.make_async_copy(src, dst, small_sem.at[i]) for i, (src, dst) in enumerate(pairs)
    ]
    for copy in small:
        copy.start()
    for q in range(parts):
        load(q).start()
    rows_copy = pltpu.make_async_copy(rows_hbm, rows_sm, rows_sem)
    rows_copy.start()

    def across(j):
        return (lax.rem(gx + j, n_gx), gy)

    barrier = pltpu.get_barrier_semaphore()

    def greet(j, carry):
        pl.semaphore_signal(barrier, inc=1, device_id=across(j), device_id_type=MESH)
        return carry

    lax.fori_loop(1, n_gx, greet, 0)

    @pl.when(gy > 0)
    def _():
        pl.semaphore_signal(barrier, inc=1, device_id=(gx, gy - 1), device_id_type=MESH)

    @pl.when(gy < n_gy - 1)
    def _():
        pl.semaphore_signal(barrier, inc=1, device_id=(gx, gy + 1), device_id_type=MESH)

    for q in range(parts):
        load(q).wait()

        def widen(i, carry):
            rows = probes_ref[i].astype(F32)
            for p in range(split):
                at = pl.ds(i * (tile_c * split) + p, tile_c, stride=split)
                tile_ref[at, :] = rows[:, p * width : (p + 1) * width]
            return carry

        lax.fori_loop(q * span, (q + 1) * span, widen, 0)
    for copy in small:
        copy.wait()
    coef32_ref[...] = coef_ref[...].astype(F32)
    slot = lax.broadcasted_iota(jnp.int32, (1, nblk), 1)
    ids_one = jnp.where(slot < count_ref[...], sensor_ref[...] + 1, 0).astype(F32)
    down = lax.broadcasted_iota(jnp.int32, (nblk, nblk), 0)
    ids_col = jnp.sum(
        jnp.where(down == lax.broadcasted_iota(jnp.int32, (nblk, nblk), 1), ids_one, 0.0),
        axis=1, keepdims=True,
    )
    offset = lax.rem(gx, share) * nblk
    ids_send[...] = jnp.sum(
        jnp.where(
            lax.broadcasted_iota(jnp.int32, (nblk, wide), 1)
            == lax.broadcasted_iota(jnp.int32, (nblk, wide), 0) + offset,
            ids_col, 0.0,
        ),
        axis=0, keepdims=True,
    )
    ids_recv[gx] = ids_send[...]

    def plane(j, carry):
        at = rows_ref[pl.ds(j, 1), :]
        c = coef32_ref[pl.ds(j, 1), :]
        square = c * c
        top = square.astype(BF16).astype(F32)
        high = at // tile_c
        low = at - high * tile_c
        here = high == lax.broadcasted_iota(jnp.int32, (tile_r, foot), 0)
        left = jnp.concatenate(
            [jnp.where(here, top, 0.0), jnp.where(here, square - top, 0.0)], axis=0
        ).astype(BF16)
        right = jnp.where(
            low == lax.broadcasted_iota(jnp.int32, (tile_c, foot), 0), 1.0, 0.0
        ).astype(BF16)
        both = lax.dot_general(left, right, NT, preferred_element_type=F32)
        planes_ref[j] = both[:tile_r] + both[tile_r:]
        return carry

    lax.fori_loop(0, FRONT, plane, 0)
    rows_copy.wait()

    def block_copy(q, g, j):
        return pltpu.make_async_remote_copy(
            src_ref=send_ref.at[q, g, across(j)[0]], dst_ref=recv_ref.at[q, g, gx],
            send_sem=send_sem, recv_sem=recv_sem.at[q, g],
            device_id=across(j), device_id_type=MESH,
        )

    def ids_copy(j):
        return pltpu.make_async_remote_copy(
            src_ref=ids_send, dst_ref=ids_recv.at[gx],
            send_sem=ids_send_sem, recv_sem=ids_recv_sem,
            device_id=across(j), device_id_type=MESH,
        )

    def part_copy(q, c, up):
        return pltpu.make_async_remote_copy(
            src_ref=part_out.at[q * items + c], dst_ref=part_in.at[q, c],
            send_sem=part_send_sem, recv_sem=part_sem.at[q, c],
            device_id=(gx, gy + up), device_id_type=MESH,
        )

    def part_x_copy(q, c, up):
        return pltpu.make_async_remote_copy(
            src_ref=part_out.at[q * items + c], dst_ref=part_x.at[q, c - first_tail],
            send_sem=part_send_sem, recv_sem=part_x_sem.at[q, c - first_tail],
            device_id=(gx, gy + up), device_id_type=MESH,
        )

    def h_peer(k):
        far = k // n_gx
        tz = jnp.where(gy < n_gy // 2, n_gy - 1 - far, far)
        tx = lax.rem(gx + lax.rem(k, n_gx), n_gx)
        return tx * n_gy + tz, (tx, tz)

    def h_copy(k):
        return pltpu.make_async_remote_copy(
            src_ref=h_send, dst_ref=h_recv.at[flat],
            send_sem=h_send_sem, recv_sem=h_recv_sem,
            device_id=h_peer(k)[1], device_id_type=MESH,
        )

    channel = lax.broadcasted_iota(jnp.int32, (nblk, foot), 1)
    batch = stage_ref.shape[0]

    def gather(q, g):
        def some(b, carry):
            for e in range(batch):
                d = b * batch + e
                r = (g * 2 + q) * n_gx + d
                column = jnp.sum(
                    jnp.where(channel == r, coef32_ref[...], 0.0), axis=1, keepdims=True
                )
                for j in range(nblk):
                    at = rows_sm[j, r] * split
                    stage_ref[e, pl.ds(j * split, split), :] = tile_ref[pl.ds(at, split), :]
                for p in range(split):
                    part = stage_ref[e, pl.ds(p, nblk, stride=split), :]
                    send_ref[q, g, d, :, p * width : (p + 1) * width] = (part * column).astype(BF16)
            return carry

        lax.fori_loop(0, n_gx // batch, some, 0)

    def launch(q, g):
        recv_ref[q, g, gx] = send_ref[q, g, gx]
        for j in range(1, n_gx):
            block_copy(q, g, j).start()

    gather(0, 0)
    pl.semaphore_wait(
        barrier,
        n_gx - 1 + jnp.where(gy > 0, 1, 0) + jnp.where(gy < n_gy - 1, 1, 0),
    )
    for j in range(1, n_gx):
        ids_copy(j).start()
    launch(0, 0)

    def gather_on(k, carry):
        gather(k % 2, k // 2)
        launch(k % 2, k // 2)
        return carry

    lax.fori_loop(1, AHEAD, gather_on, 0)

    rest = pl.ds(0, n_gx - 1)
    pltpu.make_async_copy(ids_recv.at[rest], ids_recv.at[rest], ids_recv_sem).wait()
    sensor_up = (lax.broadcasted_iota(jnp.int32, (n_sens, wide), 0) + 1).astype(F32)
    for piece in range(n_gx // share):
        row = ids_recv[piece * share]
        for extra in range(1, share):
            row = row + ids_recv[piece * share + extra]
        mixer_ref[:, piece * wide : (piece + 1) * wide] = jnp.where(
            row == sensor_up, 1.0, 0.0
        ).astype(BF16)
    acc_ref[...] = jnp.zeros_like(acc_ref)

    others = pl.ds(0, n_gx - 1)

    def mix(q, g):
        pltpu.make_async_copy(
            send_ref.at[q, g, others], recv_ref.at[q, g, others], recv_sem.at[q, g]
        ).wait()
        y = jnp.dot(
            mixer_ref[...], recv_ref[q, g].reshape(depth_k, probe_n), preferred_element_type=F32
        )
        for p in range(split):
            for v in range(stack):
                own_ref[q, (g * split + p) * stack + v] = y[
                    v * part_rows : (v + 1) * part_rows, p * width : (p + 1) * width
                ]

    def collect(q, c, f, crossing):
        below = (gy > 0) & (gy <= f)
        above = (gy < n_gy - 1) & (gy >= f)

        @pl.when(below if q == 0 else above)
        def _():
            pltpu.make_async_copy(part_out.at[0], part_in.at[q, c], part_sem.at[q, c]).wait()
            own_ref[q, c] += part_in[q, c].astype(F32)

        if crossing:
            @pl.when(above if q == 0 else below)
            def _():
                at = c - first_tail
                pltpu.make_async_copy(
                    part_out.at[0], part_x.at[q, at], part_x_sem.at[q, at]
                ).wait()
                own_ref[q, c] += part_x[q, at].astype(F32)

        @pl.when(gy == f)
        def _():
            v = lax.rem(c, stack)
            total = acc_ref[v]
            for at in range(0, width, LANES):
                y = own_ref[q, c, :, at : at + LANES]
                total = total + y * y
            acc_ref[v] = total

    def process(q, c, f, crossing, head):
        if not head:
            collect(q, c, f, crossing)

        @pl.when(gy < f)
        def _():
            part_out[q * items + c] = own_ref[q, c].astype(BF16)
            (part_copy if q == 0 else part_x_copy)(q, c, 1).start()

        @pl.when(gy > f)
        def _():
            part_out[q * items + c] = own_ref[q, c].astype(BF16)
            (part_copy if q == 1 else part_x_copy)(q, c, -1).start()

    def ends(q, crossing):
        if crossing:
            return n_gy // 2 - q
        return n_gy - 1 if q == 0 else 0

    def depth_of(f):
        low = jnp.where(gy <= f, gy, 0)
        high = jnp.where(gy >= f, n_gy - 1 - gy, 0)
        return jnp.maximum(low, high)

    late = fine // 2
    every, halves = max(1, fine // 2), max(1, 2 // fine)
    each = max(0, nblk - FRONT) // (2 * AHEAD)
    steps = items + late + LAG * (n_gy - 1)

    def turns(s, q, crossing):
        f = ends(q, crossing)
        lo, hi = (first_tail, items) if crossing else (0, first_tail)
        depth = depth_of(f)
        c = s - LAG * depth - (late if q else 0)
        return f, depth, c, (c >= lo) & (c < hi)

    kinds = (True, False) if tail else (False,)

    def chain(s):
        for crossing in kinds:
            for q in range(2):
                f, depth, c, turn = turns(s, q, crossing)

                @pl.when(turn & (depth > 0))
                def _():
                    process(q, c, f, crossing, False)

    def heads(s):
        for crossing in reversed(kinds):
            for q in range(2):
                f, depth, c, turn = turns(s, q, crossing)

                @pl.when(turn & (depth == 0) & ((gy == 0) if q == 0 else (gy > 0)))
                def _():
                    process(q, c, f, crossing, True)
        if tail:
            for q in range(2):
                f, depth, c, turn = turns(s - tail, q, True)

                @pl.when(turn & (depth == 0) & ((gy > 0) if q == 0 else (gy == 0)))
                def _():
                    process(q, c, f, True, True)

    def step(s, carry):
        chain(s)
        for e in range(halves):
            k = s // every * halves + e
            turn = lax.rem(s, every) == 0

            @pl.when(turn & (k + AHEAD < 2 * groups))
            def _():
                gather((k + AHEAD) % 2, (k + AHEAD) // 2)
                launch((k + AHEAD) % 2, (k + AHEAD) // 2)

            @pl.when(turn & (k + AHEAD >= 2 * groups) & (k < 2 * groups))
            def _():
                for b in range(each):
                    plane(FRONT + (k + AHEAD - 2 * groups) * each + b, 0)

            @pl.when(turn & (k < 2 * groups))
            def _():
                mix(k % 2, k // 2)

        heads(s)
        return carry

    lax.fori_loop(0, steps, step, 0)

    h_send[...] = lax.dot_general(
        jnp.ones((8, LANES), F32), acc_ref[...].reshape(n_sens, LANES), NT,
        precision=lax.Precision.HIGHEST, preferred_element_type=F32,
    )[0:1]
    h_recv[flat] = h_send[...]

    def h_launch(k, carry):
        @pl.when(h_peer(k)[0] != flat)
        def _():
            h_copy(k).start()
        return carry

    lax.fori_loop(0, n, h_launch, 0)
    lax.fori_loop(FRONT + AHEAD * each, nblk, plane, 0)

    spd = n_sens // n
    mine = jnp.where(owner_ref[...] == flat, 1.0, 0.0)
    before = jnp.where(
        lax.broadcasted_iota(jnp.int32, (n_sens, n_sens), 0)
        < lax.broadcasted_iota(jnp.int32, (n_sens, n_sens), 1),
        1.0, 0.0,
    ).astype(BF16)
    rank = jnp.dot(
        jnp.broadcast_to(mine, (spd, n_sens)).astype(BF16), before, preferred_element_type=F32
    )
    place = lax.broadcasted_iota(jnp.int32, (spd, n_sens), 0).astype(F32)
    select = jnp.where(rank == place, 1.0, 0.0) * mine

    def drain(count):
        sent = pl.ds(0, 2 * items - count)
        pltpu.make_async_copy(part_out.at[sent], part_out.at[sent], part_send_sem).wait()

    middle = (gy == n_gy // 2) | (gy == n_gy // 2 - 1)
    edge = (gy == 0) | (gy == n_gy - 1)
    pl.when(edge)(lambda: drain(first_tail))
    pl.when(middle & jnp.logical_not(edge))(lambda: drain(tail))
    pl.when(jnp.logical_not(middle | edge))(lambda: drain(0))
    whole = pl.ds(0, n_gx - 1)
    pltpu.make_async_copy(
        send_ref.at[:, :, whole], recv_ref.at[:, :, whole], send_sem
    ).wait()
    pltpu.make_async_copy(ids_recv.at[rest], ids_recv.at[rest], ids_send_sem).wait()

    peers = h_recv.at[pl.ds(0, n - 1)]
    pltpu.make_async_copy(peers, peers, h_send_sem).wait()
    pltpu.make_async_copy(peers, peers, h_recv_sem).wait()
    h = jnp.sum(h_recv[...], axis=0) * scale
    gain = weights_ref[...] * jnp.sqrt(1.0 + h)
    new = n_sens * gain / jnp.sum(gain, axis=1, keepdims=True)
    new_ref[...] = new
    owned = jnp.sum(select * h, axis=1, keepdims=True)
    small = lax.broadcasted_iota(jnp.int32, (spd, spd), 0) == lax.broadcasted_iota(
        jnp.int32, (spd, spd), 1
    )
    owned_ref[...] = jnp.sum(jnp.where(small, owned, 0.0), axis=0, keepdims=True)
    lookup = ids_col == (lax.broadcasted_iota(jnp.int32, (nblk, n_sens), 1) + 1).astype(F32)
    factor = jnp.sum(jnp.where(lookup, new, 0.0), axis=1, keepdims=True)
    total = factor[0:1] * planes_ref[0]
    for j in range(1, nblk):
        total = total + factor[j : j + 1] * planes_ref[j]
    density_ref[...] = total
    results = (
        (owned_ref, owned_hbm), (new_ref, new_hbm), (density_ref, density_hbm),
    )
    out = [pltpu.make_async_copy(src, dst, out_sem.at[i]) for i, (src, dst) in enumerate(results)]
    for copy in out:
        copy.start()
    for copy in out:
        copy.wait()


def write_kernel(owned_in, new_in, density_in, owned_ref, new_ref, density_ref):
    owned_ref[...] = owned_in[...]
    new_ref[...] = new_in[...]
    density_ref[...] = density_in[...]


def local(n_gx, n_gy, probes, blk_rows, blk_sensor, blk_count, coef, owner, weights):
    tile_r, tile_c, probe_n = probes.shape
    nblk, foot = blk_rows.shape
    n_sens = owner.shape[0]
    n = n_gx * n_gy
    width = LANES
    groups, split = foot // n_gx // 2, probe_n // width
    stack = STACK
    part_rows = n_sens // stack
    items = groups * split * stack
    tail = TAIL * items // 32 if n_gy > 3 else 0
    wide = max(LANES, nblk)
    batch = min(n_gx, max(1, 256 // nblk))

    vmem = pl.BlockSpec(memory_space=pltpu.VMEM)
    hbm = pl.BlockSpec(memory_space=pltpu.HBM)
    dma = pltpu.SemaphoreType.DMA
    outs = (
        jax.ShapeDtypeStruct((1, n_sens // n), F32),
        jax.ShapeDtypeStruct((1, n_sens), F32),
        jax.ShapeDtypeStruct((tile_r, tile_c), F32),
    )
    results = pl.pallas_call(
        functools.partial(step_kernel, n_gx, n_gy, 1.0 / (foot * probe_n), tail),
        out_shape=outs,
        in_specs=[hbm] * 7,
        out_specs=(hbm, hbm, hbm),
        scratch_shapes=[
            pltpu.VMEM((1, 1), jnp.int32),
            pltpu.VMEM((1, nblk), jnp.int32),
            pltpu.VMEM((nblk, foot), jnp.int32),
            pltpu.VMEM((nblk, foot), BF16),
            pltpu.VMEM((1, n_sens), jnp.int32),
            pltpu.VMEM((1, n_sens), F32),
            pltpu.VMEM((1, n_sens // n), F32),
            pltpu.VMEM((1, n_sens), F32),
            pltpu.VMEM((tile_r, tile_c), F32),
            dma((6,)), dma((3,)),
            pltpu.SMEM((nblk, foot), jnp.int32),
            pltpu.VMEM((tile_r, tile_c, probe_n), BF16),
            pltpu.VMEM((tile_r * tile_c * split, width), F32),
            pltpu.VMEM((batch, nblk * split, width), F32),
            pltpu.VMEM((nblk, foot), F32),
            pltpu.VMEM((2, groups, n_gx, nblk, probe_n), BF16),
            pltpu.VMEM((2, groups, n_gx, nblk, probe_n), BF16),
            pltpu.VMEM((1, wide), F32),
            pltpu.VMEM((n_gx, 1, wide), F32),
            pltpu.VMEM((n_sens, n_gx * nblk), BF16),
            pltpu.VMEM((2, items, part_rows, width), F32),
            pltpu.VMEM((2 * items, part_rows, width), BF16),
            pltpu.VMEM((2, items, part_rows, width), BF16),
            pltpu.VMEM((2, max(1, tail), part_rows, width), BF16),
            pltpu.VMEM((stack, part_rows, LANES), F32),
            pltpu.VMEM((nblk, tile_r, tile_c), F32),
            pltpu.VMEM((1, n_sens), F32),
            pltpu.VMEM((n, 1, n_sens), F32),
            dma, dma((4,)), dma, dma((2, groups)), dma, dma, dma,
            dma((2, items)), dma((2, max(1, tail))), dma, dma,
        ],
        compiler_params=pltpu.CompilerParams(
            collective_id=0, has_side_effects=True, vmem_limit_bytes=60 * 2**20
        ),
        name="reweight_step",
    )(
        blk_rows, probes, blk_count.reshape(1, 1), blk_sensor.reshape(1, nblk), coef,
        owner.reshape(1, n_sens), weights.reshape(1, n_sens),
    )
    owned, new, density = pl.pallas_call(
        write_kernel,
        out_shape=outs,
        in_specs=[vmem] * 3,
        out_specs=(vmem,) * 3,
        name="write_results",
    )(*results)
    return owned.reshape(-1), new.reshape(-1), density


def solution(mesh):
    n_gx, n_gy = mesh.shape["gx"], mesh.shape["gy"]
    in_specs = (
        P("gx", "gy", None),
        P(("gx", "gy"), None),
        P(("gx", "gy")),
        P(("gx", "gy")),
        P(("gx", "gy"), None),
        P(),
        P(),
    )
    out_specs = (P(("gx", "gy")), P(), P("gx", "gy"))
    return jax.shard_map(
        functools.partial(local, n_gx, n_gy),
        mesh=mesh, in_specs=in_specs, out_specs=out_specs, check_vma=False,
    )
```

time: 57.9 us -> 49.9 us (0.86)
  Pallas kernels: 52.6 us -> 48.4 us
  local copies, waits for them, and re-layouts: 3.75 us -> 0 us
    pallas_call x1, Pallas kernels: 52.6 us -> 47 us  [local(): pl.pallas_call(functools.partial(step_kernel, n_gx, n_gy, 1.0 / (foot * p...]
    unnamed x3 -> x0, local copies, waits for them, and re-layouts: 3.75 us -> none
    pallas_call x0 -> x1, Pallas kernels: none -> 1.39 us  [local(): pl.pallas_call(write_kernel, out_shape=outs, in_specs=[vmem] * 3, out_spe...]
where the time goes in v2:
time: 49.9 us; the launch traced here: 49.7 us
  Pallas kernels  48.4 us (97%)
  between operations  1.29 us (3%)
    pallas_call x1, Pallas kernels, local(): pl.pallas_call(functools.partial(step_kernel, n_gx, n_gy, 1.0 / (foot * p...  47 us
    pallas_call x1, Pallas kernels, local(): pl.pallas_call(write_kernel, out_shape=outs, in_specs=[vmem] * 3, out_spe...  1.39 us

profile of v2, /device:TPU:0, one launch (start us, length us, event | category | flops | bytes accessed | tf_op | source)
XLA Modules:
  0.0 49.7 jit_solution(17917829246932533827)
XLA Ops:
  1.3 47.0 %reweight_step.1 = (f32[1,8]{1,0:T(1,128)}, f32[1,256]{1,0:T(1,128)}, f32[32,256]{1,0:T(8,128)}) custom-call(s32[32,128]{1,0:T(8,128)} %rows_hbm.1, bf16[32,256,256]{2,1,0:T(8,128)(2,1)} %probes_hbm.1, s32[1,1]{1,0:T(1,128)} %bitcast.6.count_hbm, s32[1,32]{1,0:T(1,128)} %bitcast.9, bf16[32,128]{1,0:T(8,128)(2,1)} %coef_hbm.1, s32[1,256]{1,0:T(1,128)} %bitcast.7, ...), custom_call_target="tpu_custom_call" | custom-call | tf_op jit(solution)/shard_map/reweight_step/pallas_call | solution.py:467
  48.3 1.4 %write_results.1 = (f32[1,8]{1,0:T(1,128)}, f32[1,256]{1,0:T(1,128)}, f32[32,256]{1,0:T(8,128)}) custom-call(f32[1,8]{1,0:T(1,128)} %get-tuple-element.9.owned_in, f32[1,256]{1,0:T(1,128)} %get-tuple-element.10.new_in, f32[32,256]{1,0:T(8,128)} %get-tuple-element.11.density_in), custom_call_target="tpu_custom_call" | custom-call | tf_op jit(solution)/shard_map/write_results/pallas_call | solution.py:512

commit v3 on v2

--- a/solution.py
+++ b/solution.py
@@ -22,9 +22,9 @@
 def step_kernel(
     n_gx, n_gy, scale, tail,
     rows_hbm, probes_hbm, count_hbm, sensor_hbm, coef_hbm, owner_hbm, weights_hbm,
-    owned_hbm, new_hbm, density_hbm,
+    owned_ref, new_ref, density_ref,
     count_ref, sensor_ref, rows_ref, coef_ref, owner_ref, weights_ref,
-    owned_ref, new_ref, density_ref, small_sem, out_sem,
+    small_sem,
     rows_sm, probes_ref, tile_ref, stage_ref, coef32_ref, send_ref, recv_ref, ids_send, ids_recv,
     mixer_ref, own_ref, part_out, part_in, part_x, acc_ref, planes_ref, h_send, h_recv,
     rows_sem, load_sem, send_sem, recv_sem, ids_send_sem, ids_recv_sem, part_send_sem,
@@ -426,14 +426,6 @@
     for j in range(1, nblk):
         total = total + factor[j : j + 1] * planes_ref[j]
     density_ref[...] = total
-    results = (
-        (owned_ref, owned_hbm), (new_ref, new_hbm), (density_ref, density_hbm),
-    )
-    out = [pltpu.make_async_copy(src, dst, out_sem.at[i]) for i, (src, dst) in enumerate(results)]
-    for copy in out:
-        copy.start()
-    for copy in out:
-        copy.wait()
 
 
 def write_kernel(owned_in, new_in, density_in, owned_ref, new_ref, density_ref):
@@ -466,9 +458,9 @@
     )
     results = pl.pallas_call(
         functools.partial(step_kernel, n_gx, n_gy, 1.0 / (foot * probe_n), tail),
-        out_shape=outs,
+        out_shape=tuple(pltpu.VMEM(out.shape, out.dtype) for out in outs),
         in_specs=[hbm] * 7,
-        out_specs=(hbm, hbm, hbm),
+        out_specs=(vmem,) * 3,
         scratch_shapes=[
             pltpu.VMEM((1, 1), jnp.int32),
             pltpu.VMEM((1, nblk), jnp.int32),
@@ -476,10 +468,7 @@
             pltpu.VMEM((nblk, foot), BF16),
             pltpu.VMEM((1, n_sens), jnp.int32),
             pltpu.VMEM((1, n_sens), F32),
-            pltpu.VMEM((1, n_sens // n), F32),
-            pltpu.VMEM((1, n_sens), F32),
-            pltpu.VMEM((tile_r, tile_c), F32),
-            dma((6,)), dma((3,)),
+            dma((6,)),
             pltpu.SMEM((nblk, foot), jnp.int32),
             pltpu.VMEM((tile_r, tile_c, probe_n), BF16),
             pltpu.VMEM((tile_r * tile_c * split, width), F32),
@@ -515,7 +504,7 @@
         in_specs=[vmem] * 3,
         out_specs=(vmem,) * 3,
         name="write_results",
-    )(*results)
+    )(*[pltpu.with_memory_space_constraint(r, pltpu.VMEM) for r in results])
     return owned.reshape(-1), new.reshape(-1), density
 
 

time: 49.9 us -> 48.5 us (0.972)
  Pallas kernels: 48.4 us -> 47 us
    pallas_call x1, Pallas kernels: 1.39 us -> 0.63 us  [local(): pl.pallas_call(write_kernel, out_shape=outs, in_specs=[vmem] * 3, out_spe...]
    pallas_call x1, Pallas kernels: 47 us -> 46.4 us  [local(): pl.pallas_call(functools.partial(step_kernel, n_gx, n_gy, 1.0 / (foot * p...]
where the time goes in v3:
time: 48.5 us; the launch traced here: 48.3 us
  Pallas kernels  47 us (97%)
  between operations  1.29 us (3%)
    pallas_call x1, Pallas kernels, local(): pl.pallas_call(functools.partial(step_kernel, n_gx, n_gy, 1.0 / (foot * p...  46.4 us

profile of v3, /device:TPU:0, one launch (start us, length us, event | category | flops | bytes accessed | tf_op | source)
XLA Modules:
  0.0 48.3 jit_solution(13153064936485029580)
XLA Ops:
  1.3 46.4 %reweight_step.1 = (f32[1,8]{1,0:T(1,128)S(1)}, f32[1,256]{1,0:T(1,128)S(1)}, f32[32,256]{1,0:T(8,128)S(1)}) custom-call(s32[32,128]{1,0:T(8,128)} %rows_hbm.1, bf16[32,256,256]{2,1,0:T(8,128)(2,1)} %probes_hbm.1, s32[1,1]{1,0:T(1,128)} %bitcast.6.count_hbm, s32[1,32]{1,0:T(1,128)} %bitcast.9, bf16[32,128]{1,0:T(8,128)(2,1)} %coef_hbm.1, s32[1,256]{1,0:T(1,128)} %bitcast.7, ...), custom_call_target="tpu_custom_call" | custom-call | tf_op jit(solution)/shard_map/reweight_step/pallas_call | solution.py:459
  47.7 0.6 %write_results.1 = (f32[1,8]{1,0:T(1,128)}, f32[1,256]{1,0:T(1,128)}, f32[32,256]{1,0:T(8,128)}) custom-call(f32[1,8]{1,0:T(1,128)S(1)} %get-tuple-element.9.owned_in, f32[1,256]{1,0:T(1,128)S(1)} %get-tuple-element.10.new_in, f32[32,256]{1,0:T(8,128)S(1)} %get-tuple-element.11.density_in), custom_call_target="tpu_custom_call" | custom-call | tf_op jit(solution)/shard_map/write_results/pallas_call | solution.py:501

commit v4 on v3

--- a/solution.py
+++ b/solution.py
@@ -15,7 +15,7 @@
 LAG = 3
 STACK = 1
 TAIL = 4
-AHEAD = 6
+AHEAD = 5
 FRONT = 0
 
 
@@ -207,13 +207,13 @@
         for j in range(1, n_gx):
             block_copy(q, g, j).start()
 
-    gather(0, 0)
     pl.semaphore_wait(
         barrier,
         n_gx - 1 + jnp.where(gy > 0, 1, 0) + jnp.where(gy < n_gy - 1, 1, 0),
     )
     for j in range(1, n_gx):
         ids_copy(j).start()
+    gather(0, 0)
     launch(0, 0)
 
     def gather_on(k, carry):
@@ -316,7 +316,7 @@
     kinds = (True, False) if tail else (False,)
 
     def chain(s):
-        for crossing in kinds:
+        for crossing in reversed(kinds):
             for q in range(2):
                 f, depth, c, turn = turns(s, q, crossing)
 

time: 48.5 us -> 48.3 us (level)
  no operation moved by 1% of the time
where the time goes in v4:
time: 48.3 us; the launch traced here: 48.2 us
  Pallas kernels  46.9 us (97%)
  between operations  1.29 us (3%)
    pallas_call x1, Pallas kernels, local(): pl.pallas_call(functools.partial(step_kernel, n_gx, n_gy, 1.0 / (foot * p...  46.3 us

profile of v4, /device:TPU:0, one launch (start us, length us, event | category | flops | bytes accessed | tf_op | source)
XLA Modules:
  0.0 48.2 jit_solution(1085906431711820622)
XLA Ops:
  1.3 46.3 %reweight_step.1 = (f32[1,8]{1,0:T(1,128)S(1)}, f32[1,256]{1,0:T(1,128)S(1)}, f32[32,256]{1,0:T(8,128)S(1)}) custom-call(s32[32,128]{1,0:T(8,128)} %rows_hbm.1, bf16[32,256,256]{2,1,0:T(8,128)(2,1)} %probes_hbm.1, s32[1,1]{1,0:T(1,128)} %bitcast.6.count_hbm, s32[1,32]{1,0:T(1,128)} %bitcast.9, bf16[32,128]{1,0:T(8,128)(2,1)} %coef_hbm.1, s32[1,256]{1,0:T(1,128)} %bitcast.7, ...), custom_call_target="tpu_custom_call" | custom-call | tf_op jit(solution)/shard_map/reweight_step/pallas_call | solution.py:459
  47.5 0.6 %write_results.1 = (f32[1,8]{1,0:T(1,128)}, f32[1,256]{1,0:T(1,128)}, f32[32,256]{1,0:T(8,128)}) custom-call(f32[1,8]{1,0:T(1,128)S(1)} %get-tuple-element.9.owned_in, f32[1,256]{1,0:T(1,128)S(1)} %get-tuple-element.10.new_in, f32[32,256]{1,0:T(8,128)S(1)} %get-tuple-element.11.density_in), custom_call_target="tpu_custom_call" | custom-call | tf_op jit(solution)/shard_map/write_results/pallas_call | solution.py:501
